TPU v7x, 32 devices: a whole 2x2x4 slice. The times are simulated.
32 devices in a mesh: dp: 4 (over z), neg: 8 (over y, x, core).
Axes of the slice: x: 2, y: 2, z: 4, core: 2. Of those that a mesh axis runs over, the one named last changes fastest.
Arguments:
- query_emb: bfloat16 [128, 32, 128], P(('dp', 'neg')), may hold values from -6 to 6
- positive: int32 [128], P(('dp', 'neg')), may hold values from 0 to 31
- passage_emb: bfloat16 [32, 512, 128], P(('dp', 'neg')), may hold values from -6 to 6
- lengths: int32 [32], P(('dp', 'neg')), may hold values from 256 to 512
- residual: bfloat16 [16384, 1024], P(('dp', 'neg')), may hold values from -6 to 6
- context: bfloat16 [16384, 1024], P(('dp', 'neg')), may hold values from -6 to 6
- out_proj: bfloat16 [1024, 1024], replicated, may hold values from -0.1875 to 0.1875
- norm_gain: float32 [1024], replicated, may hold values from 0.5 to 1.5
- colbert_proj: bfloat16 [1024, 128], replicated, may hold values from -0.1875 to 0.1875
Outputs:
- loss: float32 [], replicated
- query_grad: float32 [128, 32, 128], P(('dp', 'neg'))
- residual_grad: bfloat16 [16384, 1024], P(('dp', 'neg'))
- context_grad: bfloat16 [16384, 1024], P(('dp', 'neg'))
- out_proj_grad: float32 [1024, 1024], replicated
- colbert_grad: float32 [1024, 128], replicated
- gain_grad: float32 [1024], replicated
Inputs may be any that keep to these rules, and one draw needn't show every extreme that they name: A passage's first lengths[p] token slots are real, the rest padding.
All inputs are finite; a program needn't handle non-finite values.
Results may differ from a plain program's by a relative error of at most 0.0065.
Values may be sent and summed in bfloat16 or wider, within the bound.
A program may use at most 64 MiB of HBM per device.

v0:
```python
import math
import jax
import jax.numpy as jnp
from jax import lax
from jax.sharding import PartitionSpec as P


def combined_all(array, axis, combine):
    everything = jax.tree.map(lambda part: lax.all_gather(part, axis), array)
    initial = jax.tree.map(lambda part: part[0], everything)

    def turn(k, so_far):
        return combine(so_far, jax.tree.map(lambda part: part[k], everything))

    return lax.fori_loop(1, lax.axis_size(axis), turn, initial)


def block_plan(query_count, query_len):
    return math.gcd(query_count, max(1, 2048 // query_len))


def masked_scores(query_block, passage_one, usable):
    scores = jnp.einsum("rd,jd->rj", query_block, passage_one, preferred_element_type=jnp.float32)
    return jnp.where(usable, scores, -1e30)


def tile_forward(query_tokens, query_pos, passage_tokens, passage_len, passage_ids):
    query_count, query_len, emb_width = query_tokens.shape
    per_block = block_plan(query_count, query_len)
    query_blocks = query_tokens.reshape(query_count // per_block, per_block * query_len, emb_width)

    def per_passage(inputs):
        passage_one, length = inputs
        usable = (jnp.arange(passage_one.shape[0]) < length)[None, :]

        def per_query(query_block):
            masked = masked_scores(query_block, passage_one, usable)
            highest = jnp.max(masked, axis=1, keepdims=True)
            return highest[:, 0] + jnp.log(jnp.sum(jnp.exp(masked - highest), axis=1))

        inner_lse = lax.map(per_query, query_blocks).reshape(query_count, query_len)
        shifted = inner_lse - jnp.log(length.astype(jnp.float32))
        return (inner_lse, jnp.sum(shifted, axis=1))

    inner_all, similar = lax.map(per_passage, (passage_tokens, passage_len))
    similar = similar.T
    is_positive = passage_ids[None, :] == query_pos[:, None]
    highest = jnp.max(similar, axis=1)
    exp_total = jnp.sum(jnp.exp(similar - highest[:, None]), axis=1)
    positive_score = jnp.sum(jnp.where(is_positive, similar, 0.0), axis=1)
    return (inner_all, similar, is_positive, (highest, exp_total, positive_score))


def combine_totals(earlier, later):
    highest = jnp.maximum(earlier[0], later[0])
    exp_total = earlier[1] * jnp.exp(earlier[0] - highest) + later[1] * jnp.exp(later[0] - highest)
    return (highest, exp_total, earlier[2] + later[2])


def finish_rows(similar, is_positive, totals, own_block, query_dev):
    log_total = totals[0] + jnp.log(totals[1])
    coefficient = jnp.exp(similar - log_total[:, None]) - is_positive.astype(jnp.float32)
    own_terms = lax.dynamic_slice_in_dim(log_total - totals[2], own_block * query_dev, query_dev)
    return (coefficient, jnp.sum(own_terms))


def tile_backward(query_tokens, passage_tokens, passage_len, inner_all, coefficient):
    query_count, query_len, emb_width = query_tokens.shape
    per_block = block_plan(query_count, query_len)
    block_count = query_count // per_block
    query_blocks = query_tokens.reshape(block_count, per_block * query_len, emb_width)

    def per_passage(running, inputs):
        passage_one, length, inner_lse, column = inputs
        usable = (jnp.arange(passage_one.shape[0]) < length)[None, :]

        def per_query(pieces):
            query_block, inner_block, column_block = pieces
            masked = masked_scores(query_block, passage_one, usable)
            spread = jnp.exp(masked - inner_block.reshape(-1)[:, None]).reshape(
                per_block, query_len, -1
            )
            weight = (
                (spread * column_block[:, None, None])
                .reshape(per_block * query_len, -1)
                .astype(jnp.bfloat16)
            )
            query_part = jnp.dot(weight, passage_one, preferred_element_type=jnp.float32)
            passage_part = jnp.einsum(
                "rj,rd->jd", weight, query_block, preferred_element_type=jnp.float32
            )
            return (query_part, passage_part)

        query_parts, passage_parts = lax.map(
            per_query,
            (
                query_blocks,
                inner_lse.reshape(block_count, per_block, query_len),
                column.reshape(block_count, per_block),
            ),
        )
        return (running + query_parts.reshape(running.shape), jnp.sum(passage_parts, axis=0))

    start = jnp.zeros((query_count * query_len, emb_width), jnp.float32)
    query_sum, passage_sum = lax.scan(
        per_passage, start, (passage_tokens, passage_len, inner_all, coefficient.T)
    )
    return (query_sum.reshape(query_count, query_len, emb_width), passage_sum)


def window_rows(resid_rows, context_rows, grad_rows, out_proj, norm_gain, colbert_proj):
    hidden = resid_rows.astype(jnp.float32) + jnp.dot(
        context_rows, out_proj, preferred_element_type=jnp.float32
    )
    row_mean = jnp.mean(hidden, axis=1, keepdims=True)
    centred = hidden - row_mean
    variance = jnp.mean(centred * centred, axis=1, keepdims=True)
    inv_std = 1.0 / jnp.sqrt(variance + 1e-05)
    normed = centred * inv_std
    scaled = (normed * norm_gain).astype(jnp.bfloat16)
    colbert_part = jnp.dot(scaled.T, grad_rows, preferred_element_type=jnp.float32)
    scaled_grad = jnp.dot(grad_rows, colbert_proj.T, preferred_element_type=jnp.float32)
    gain_part = jnp.sum(scaled_grad * normed, axis=0)
    gained = scaled_grad * norm_gain
    hidden_grad = (
        inv_std
        * (
            gained
            - jnp.mean(gained, axis=1, keepdims=True)
            - normed * jnp.mean(gained * normed, axis=1, keepdims=True)
        )
    ).astype(jnp.bfloat16)
    context_grad = jnp.dot(hidden_grad, out_proj.T, preferred_element_type=jnp.float32).astype(
        jnp.bfloat16
    )
    proj_part = jnp.dot(context_rows.T, hidden_grad, preferred_element_type=jnp.float32)
    return (hidden_grad, context_grad, proj_part, colbert_part, gain_part)


def body(
    query_emb, positive, passage_emb, lengths, residual, context, out_proj, norm_gain, colbert_proj
):
    query_dev = query_emb.shape[0]
    passage_dev = passage_emb.shape[0]
    neg_size = lax.axis_size("neg")
    neg_place = lax.axis_index("neg")
    query_tokens, query_pos = (
        lax.all_gather(query_emb, "neg", axis=0, tiled=True),
        lax.all_gather(positive, "neg", axis=0, tiled=True),
    )
    passage_tokens, passage_len = (
        lax.all_gather(passage_emb, "dp", axis=0, tiled=True),
        lax.all_gather(lengths, "dp", axis=0, tiled=True),
    )
    position = jnp.arange(passage_tokens.shape[0], dtype=jnp.int32)
    passage_ids = (
        position // passage_dev * neg_size + neg_place
    ) * passage_dev + position % passage_dev
    inner_all, similar, is_positive, stats = tile_forward(
        query_tokens, query_pos, passage_tokens, passage_len, passage_ids
    )
    totals = combined_all(stats, "neg", combine_totals)
    coefficient, loss_part = finish_rows(similar, is_positive, totals, neg_place, query_dev)
    query_sum, passage_sum = tile_backward(
        query_tokens, passage_tokens, passage_len, inner_all, coefficient
    )
    query_grad = lax.psum_scatter(query_sum, "neg", scatter_dimension=0, tiled=True)
    emb_sum = lax.psum_scatter(passage_sum, "dp", scatter_dimension=0, tiled=True)
    emb_grad = emb_sum.astype(jnp.bfloat16).reshape(
        passage_dev * emb_sum.shape[1], emb_sum.shape[2]
    )
    residual_grad, context_grad, proj_part, colbert_part, gain_part = window_rows(
        residual, context, emb_grad, out_proj, norm_gain, colbert_proj
    )
    out_proj_grad, colbert_grad, gain_grad, loss_total = lax.psum(
        (proj_part, colbert_part, gain_part, loss_part), ("dp", "neg")
    )
    loss = loss_total / (query_dev * lax.axis_size("dp") * neg_size)
    return (loss, query_grad, residual_grad, context_grad, out_proj_grad, colbert_grad, gain_grad)


def solution(mesh):
    in_specs = (
        P(("dp", "neg"), None, None),
        P(("dp", "neg")),
        P(("dp", "neg"), None, None),
        P(("dp", "neg")),
        P(("dp", "neg"), None),
        P(("dp", "neg"), None),
        P(),
        P(),
        P(),
    )
    out_specs = (
        P(),
        P(("dp", "neg"), None, None),
        P(("dp", "neg"), None),
        P(("dp", "neg"), None),
        P(),
        P(),
        P(),
    )
    return jax.shard_map(body, mesh=mesh, in_specs=in_specs, out_specs=out_specs, check_vma=False)
```

profile of v0, /device:TPU:0, one launch (start us, length us, event | category | flops | bytes accessed | tf_op | source)
XLA Modules:
  0.0 304.9 jit_solution(8071022490365719969)
XLA Ops:
  8.9 1.2 dynamic-slice
  10.1 0.8 dynamic-update-slice
  10.9 9.9 %all-reduce = s32[4]{0:T(128)S(1)} all-reduce(s32[4]{0:T(128)S(1)} %dynamic-update-slice), channel_id=1, replica_groups=mesh['dp'=4,'neg'=8] {'dp'}, use_global_device_ids=true, to_apply=%add | all-reduce | flops 4 | bytes 32
  20.8 16.9 %all_gather.31 = bf16[4,512,128]{2,1,0:T(8,128)(2,1)} all-gather(bf16[1,512,128]{2,1,0:T(8,128)(2,1)} %param.17), channel_id=1, replica_groups=mesh['dp'=4,'neg'=8] {'dp'}, dimensions={0}, use_global_device_ids=true | all-gather | bytes 655360 | tf_op jit(solution)/shard_map/all_gather | solution.py:152
  37.7 9.5 %all_gather.32 = bf16[32,32,128]{2,1,0:T(8,128)(2,1)S(1)} all-gather(bf16[4,32,128]{2,1,0:T(8,128)(2,1)} %param.15), channel_id=1, replica_groups=mesh['dp'=4,'neg'=8] {'neg'}, dimensions={0}, use_global_device_ids=true | all-gather | bytes 294912 | tf_op jit(solution)/shard_map/all_gather | solution.py:148
  47.2 16.2 %while.53 = (s32[]{:T(128)}, f32[4,32,32]{2,1,0:T(8,128)S(1)}, f32[4,32]{1,0:T(4,128)S(1)}, s32[4]{0:T(128)S(1)}, bf16[4,512,128]{2,1,0:T(8,128)(2,1)}, /*index=...) while((s32[]{:T(128)}, f32[4,32,32]{2,1,0:T(8,128)S(1)}, f32[4,32]{1,0:T(4,128)S(1)}, ...), condition=%wide.region_4.5_spmd, body=%wide.region_0.4_spmd.sunk | while | flops 136840672 | bytes 4672013 | solution.py:45
  47.8 0.6 iota_compare_fusion.4
  48.4 1.4 select_reduce_fusion.2
  51.8 0.6 iota_compare_fusion.4
  52.5 1.4 select_reduce_fusion.2
  55.9 0.6 iota_compare_fusion.4
  56.5 1.4 select_reduce_fusion.2
  59.9 0.6 iota_compare_fusion.4
  60.6 1.4 select_reduce_fusion.2
  64.9 7.1 %all-reduce.3 = s32[32]{0:T(128)S(1)} all-reduce(s32[32]{0:T(128)S(1)} %dynamic-update-slice.3), channel_id=1, replica_groups=mesh['dp'=4,'neg'=8] {'neg'}, use_global_device_ids=true, to_apply=%add.3 | all-reduce | flops 32 | bytes 256
  73.4 11.8 %all-reduce.7 = (f32[256]{0:T(256)S(1)}, f32[256]{0:T(256)S(1)}, f32[256]{0:T(256)S(1)}) all-reduce(f32[256]{0:T(256)S(1)} %dynamic-update-slice.1, f32[256]{0:T(256)S(1)} %dynamic-update-slice.2, f32[256]{0:T(256)S(1)} %dynamic-update-slice.4), channel_id=2, replica_groups=mesh['dp'=4,'neg'=8] {'neg'}, use_global_device_ids=true, to_apply=%add.1 | all-reduce | flops 768 | bytes 6144
  85.8 25.8 %while.55 = (s32[]{:T(128)}, f32[1024,128]{1,0:T(8,128)}, f32[4,512,128]{2,1,0:T(8,128)}, s32[4]{0:T(128)S(1)}, bf16[4,512,128]{2,1,0:T(8,128)(2,1)}, /*index=5*...) while((s32[]{:T(128)}, f32[1024,128]{1,0:T(8,128)}, ...), condition=%wide.region_13.14_spmd.clone, body=%wide.region_12.13_spmd.clone.sunk | while | flops 405012992 | bytes 5282823 | solution.py:105
  86.1 0.6 dynamic_slice.125
  86.7 0.6 iota_compare_fusion.5
  87.3 1.5 multiply_convert_fusion.5
  88.8 1.2 fusion.63
  90.0 2.2 convolution_add_fusion.2
  93.0 0.6 iota_compare_fusion.5
  93.6 1.5 multiply_convert_fusion.5
  95.1 1.1 fusion.63
  96.2 2.4 convolution_add_fusion.2
  99.4 0.6 iota_compare_fusion.5
  100.1 1.5 multiply_convert_fusion.5
  101.6 1.1 fusion.63
  102.7 2.4 convolution_add_fusion.2
  105.9 0.6 iota_compare_fusion.5
  106.6 1.5 multiply_convert_fusion.5
  108.1 1.1 fusion.63
  109.2 2.4 convolution_add_fusion.2
  111.7 2.9 fusion.36
  114.6 1.3 copy-done.1
  116.2 21.0 %reduce-scatter.5.cloned.1.call-done = f32[1,512,128]{2,1,0:T(8,128)} async-done(((f32[4,512,128]{2,1,0:T(8,128)}), f32[1,512,128]{2,1,0:T(8,128)}) %reduce-scatter.5.cloned.1.call-update) | async-done | bytes 262160 | tf_op jit(solution)/shard_map/reduce_scatter | solution.py:168
  137.3 2.7 multiply_reduce_fusion
  140.0 0.6 multiply_convert_fusion.2
  140.6 0.6 copy-done.5
  141.2 3.3 %convolution_bitcast_fusion.1 = f32[1024,1024]{0,1:T(8,128)} fusion(bf16[512,1024]{1,0:T(8,128)(2,1)S(1)} %multiply_convert_fusion.2, bf16[512,1024]{1,0:T(8,128)(2,1)S(1)} %copy-done.5), kind=kOutput, calls=%fused_computation.37 | convolution fusion | flops 1073741824 | bytes 6291456 | tf_op jit(solution)/shard_map/dot_general | solution.py:136
  144.5 1.6 fusion.22
  146.7 0.7 dynamic-slice_reduce_fusion
  147.4 39.7 %all-reduce.5 = (f32[]{:T(128)}, f32[1024]{0:T(1024)}) all-reduce(f32[]{:T(128)} %dynamic-slice_reduce_fusion, f32[1024]{0:T(1024)S(1)} %get-tuple-element.355), channel_id=1, replica_groups=mesh['dp'=4,'neg'=8] {'dp','neg'}, use_global_device_ids=true, to_apply=%region_11.12 | all-reduce | flops 1025 | bytes 8200 | tf_op jit(solution)/shard_map/psum | solution.py:175
  187.7 2.3 convolution_convert_fusion
  190.0 100.1 %all-reduce.10.cloned.1.call-done = (f32[1024,1024]{0,1:T(8,128)}, f32[1024,128]{1,0:T(8,128)}) async-done(((f32[1024,1024]{0,1:T(8,128)}, f32[1024,128]{1,0:T(8,128)}), (f32[1024,1024]{0,1:T(8,128)}, f32[1024,128]{1,0:T(8,128)})) %all-reduce.10.cloned.1.call-update) | async-done | bytes 4718608 | tf_op jit(solution)/shard_map/psum | solution.py:175
  290.1 5.4 %copy.18 = f32[1024,1024]{1,0:T(8,128)} copy(f32[1024,1024]{0,1:T(8,128)} %get-tuple-element.404) | data formatting | bytes 8388608
  295.5 0.8 copy.61
  (119 shorter events, 11.5 us)
Async XLA Ops:
  8.0 103.7 %copy-start = (bf16[1024,1024]{1,0:T(8,128)(2,1)S(1)}, bf16[1024,1024]{1,0:T(8,128)(2,1)}, u32[]{:S(2)}) copy-start(bf16[1024,1024]{1,0:T(8,128)(2,1)} %param.21) | copy-start | bytes 6291460
  8.0 129.2 %reduce-scatter.5.cloned.1.call-start = ((), (), s32[]{:S(2)}) async-start(), calls=%async_computation.3 | async-start | bytes 1310720 | tf_op jit(solution)/shard_map/reduce_scatter | solution.py:168
  47.2 16.2 %copy-start.10 = (u32[32]{0:T(128)S(1)}, u32[32]{0:T(128)}, u32[]{:S(2)}) copy-start(u32[32]{0:T(128)} %constant.164) | copy-start | bytes 388
  47.2 17.5 %copy-start.9 = (s32[4]{0:T(128)S(1)}, s32[4]{0:T(128)}, u32[]{:S(2)}) copy-start(s32[4]{0:T(128)} %param.16) | copy-start | bytes 52
  111.6 178.5 %all-reduce.10.cloned.1.call-start = ((), (), s32[]{:S(2)}) async-start(), calls=%async_computation.4 | async-start | bytes 9437184 | tf_op jit(solution)/shard_map/psum | solution.py:175
  114.6 1.3 copy-start.1
  114.6 22.7 %copy-start.7 = (bf16[1024,128]{1,0:T(8,128)(2,1)S(1)}, bf16[1024,128]{1,0:T(8,128)(2,1)}, u32[]{:S(2)}) copy-start(bf16[1024,128]{1,0:T(8,128)(2,1)} %param.23) | copy-start | bytes 786436
  114.6 22.7 %copy-start.8 = (f32[1024]{0:T(1024)S(1)}, f32[1024]{0:T(1024)}, u32[]{:S(2)}) copy-start(f32[1024]{0:T(1024)} %param.22) | copy-start | bytes 12292
  137.3 2.7 copy-start.2
  140.0 1.2 copy-start.5
  141.2 46.5 %copy-start.3 = (bf16[512,1024]{1,0:T(8,128)(2,1)}, bf16[512,1024]{1,0:T(8,128)(2,1)S(1)}, u32[]{:S(2)}) copy-start(bf16[512,1024]{1,0:T(8,128)(2,1)S(1)} %multiply_convert_fusion.2) | copy-start | bytes 3145732
  141.2 3.3 %copy-start.4 = (f32[1,512,128]{2,1,0:T(8,128)S(1)}, f32[1,512,128]{2,1,0:T(8,128)}, u32[]{:S(2)}) copy-start(f32[1,512,128]{2,1,0:T(8,128)} %reduce-scatter.5.cloned.1.call-done) | copy-start | bytes 786436
  146.1 149.4 %reduce-scatter.3.cloned.1.call-start = ((), (), s32[]{:S(2)}) async-start(), calls=%async_computation.2 | async-start | bytes 589824 | tf_op jit(solution)/shard_map/reduce_scatter | solution.py:167
  290.1 5.4 %copy-start.6 = (f32[1024,128]{1,0:T(8,128)S(1)}, f32[1024,128]{1,0:T(8,128)}, u32[]{:S(2)}) copy-start(f32[1024,128]{1,0:T(8,128)} %get-tuple-element.658) | copy-start | bytes 1572868
Sparse Core Ops, SparseCore 0:
  111.7 25.4 reduce-scatter.4
  146.3 143.7 all-reduce.9
Sparse Core Ops, SparseCore 1:
  150.3 32.6 reduce-scatter.2
where the time goes:
time: 306 us; the launch traced here: 305 us
  waiting for transfers between devices  122 us (40%)
  blocking collectives  94.9 us (31%)
  matrix products  38 us (12%)
  between operations  19.5 us (6%)
  local copies, waits for them, and re-layouts  18.2 us (6%)
  other arithmetic  9.43 us (3%)
  loops' own time  3.07 us (1%)
    psum x1, waiting for transfers between devices, body(): lax.psum((proj_part, colbert_part, gain_part, loss_part), ('dp', 'neg'))  100 us
    psum x1, blocking collectives, body(): lax.psum((proj_part, colbert_part, gain_part, loss_part), ('dp', 'neg'))  39.7 us
    unnamed x3, blocking collectives  28.8 us
    reduce_scatter x1, waiting for transfers between devices, body(): lax.psum_scatter(passage_sum, 'dp', scatter_dimension=0, tiled=True)  21 us
    all_gather x1, blocking collectives, body(): lax.all_gather(passage_emb, 'dp', axis=0, tiled=True)  16.9 us
    unnamed x36, local copies, waits for them, and re-layouts  11.6 us
    dot_general x8, matrix products, masked_scores(): jnp.einsum('rd,jd->rj', query_block, passage_one, preferred_element_type=...  11.4 us
    all_gather x1, blocking collectives, body(): lax.all_gather(query_emb, 'neg', axis=0, tiled=True)  9.51 us
  transfers between devices with their start and end apart: 3, of which 2 were waited for; matrix products, arithmetic and copies ran while one was open for 4% of the time, Pallas kernels for 0%

commit v1 on v0

--- a/solution.py
+++ b/solution.py
@@ -1,8 +1,17 @@
+import functools
 import math
 import jax
 import jax.numpy as jnp
 from jax import lax
 from jax.sharding import PartitionSpec as P
+
+
+def seats_all_show(mat, ax_name, named_axis):
+    now = jax.lax.psum(mat, ax_name)
+    return jax.lax.psum(now, named_axis)
+
+
+recover_the_results = functools.partial(seats_all_show, ax_name="neg", named_axis="dp")
 
 
 def combined_all(array, axis, combine):
@@ -172,8 +181,8 @@
     residual_grad, context_grad, proj_part, colbert_part, gain_part = window_rows(
         residual, context, emb_grad, out_proj, norm_gain, colbert_proj
     )
-    out_proj_grad, colbert_grad, gain_grad, loss_total = lax.psum(
-        (proj_part, colbert_part, gain_part, loss_part), ("dp", "neg")
+    out_proj_grad, colbert_grad, gain_grad, loss_total = recover_the_results(
+        (proj_part, colbert_part, gain_part, loss_part)
     )
     loss = loss_total / (query_dev * lax.axis_size("dp") * neg_size)
     return (loss, query_grad, residual_grad, context_grad, out_proj_grad, colbert_grad, gain_grad)

time: 306 us -> 451 us (1.47)
  waiting for transfers between devices: 122 us -> 281 us
  blocking collectives: 94.9 us -> 82.6 us
    psum x1 -> x2, waiting for transfers between devices: 100 us -> 229 us  [the longest x1 143 us: seats_all_show(): return jax.lax.psum(now, named_axis)]
    reduce_scatter x1, waiting for transfers between devices: 0.01 us -> 31.2 us  [body(): lax.psum_scatter(query_sum, 'neg', scatter_dimension=0, tiled=True)]
    psum x1 -> x2, blocking collectives: 39.7 us -> 27.4 us  [the longest x1 13.7 us: seats_all_show(): now = jax.lax.psum(mat, ax_name)]
  transfers between devices with their start and end apart: 3 -> 4, of which waited for: 2 -> 4; matrix products, arithmetic and copies ran while one was open for 4% -> 3% of each run, Pallas kernels for 0% -> 0%
where the time goes in v1:
time: 451 us
  waiting for transfers between devices  281 us (62%)
  blocking collectives  82.6 us (18%)
  matrix products  38 us (8%)
  local copies, waits for them, and re-layouts  18.2 us (4%)
  between operations  17.8 us (4%)
  other arithmetic  9.43 us (2%)
    psum x1, waiting for transfers between devices, seats_all_show(): return jax.lax.psum(now, named_axis)  143 us
    psum x1, waiting for transfers between devices, seats_all_show(): now = jax.lax.psum(mat, ax_name)  85.2 us
    reduce_scatter x1, waiting for transfers between devices, body(): lax.psum_scatter(query_sum, 'neg', scatter_dimension=0, tiled=True)  31.2 us
    unnamed x3, blocking collectives  28.8 us
    reduce_scatter x1, waiting for transfers between devices, body(): lax.psum_scatter(passage_sum, 'dp', scatter_dimension=0, tiled=True)  21 us
    all_gather x1, blocking collectives, body(): lax.all_gather(passage_emb, 'dp', axis=0, tiled=True)  16.9 us
    psum x1, blocking collectives, seats_all_show(): now = jax.lax.psum(mat, ax_name)  13.7 us
    psum x1, blocking collectives, seats_all_show(): return jax.lax.psum(now, named_axis)  13.7 us
  transfers between devices with their start and end apart: 4, of which 4 were waited for; matrix products, arithmetic and copies ran while one was open for 3% of the time, Pallas kernels for 0%

profile of v1, /device:TPU:0, one launch (start us, length us, event | category | flops | bytes accessed | tf_op | source)
XLA Modules:
  0.0 450.6 jit_solution(3994956664222402439)
XLA Ops:
  8.0 1.2 dynamic-slice
  9.3 0.8 dynamic-update-slice
  10.0 9.9 %all-reduce = s32[4]{0:T(128)S(1)} all-reduce(s32[4]{0:T(128)S(1)} %dynamic-update-slice), channel_id=1, replica_groups=mesh['dp'=4,'neg'=8] {'dp'}, use_global_device_ids=true, to_apply=%add | all-reduce | flops 4 | bytes 32
  20.0 16.9 %all_gather.31 = bf16[4,512,128]{2,1,0:T(8,128)(2,1)} all-gather(bf16[1,512,128]{2,1,0:T(8,128)(2,1)} %param.17), channel_id=1, replica_groups=mesh['dp'=4,'neg'=8] {'dp'}, dimensions={0}, use_global_device_ids=true | all-gather | bytes 655360 | tf_op jit(solution)/shard_map/all_gather | solution.py:161
  36.8 9.5 %all_gather.32 = bf16[32,32,128]{2,1,0:T(8,128)(2,1)S(1)} all-gather(bf16[4,32,128]{2,1,0:T(8,128)(2,1)} %param.15), channel_id=1, replica_groups=mesh['dp'=4,'neg'=8] {'neg'}, dimensions={0}, use_global_device_ids=true | all-gather | bytes 294912 | tf_op jit(solution)/shard_map/all_gather | solution.py:157
  46.3 16.2 %while.53 = (s32[]{:T(128)}, f32[4,32,32]{2,1,0:T(8,128)S(1)}, f32[4,32]{1,0:T(4,128)S(1)}, s32[4]{0:T(128)S(1)}, bf16[4,512,128]{2,1,0:T(8,128)(2,1)}, /*index=...) while((s32[]{:T(128)}, f32[4,32,32]{2,1,0:T(8,128)S(1)}, f32[4,32]{1,0:T(4,128)S(1)}, ...), condition=%wide.region_4.5_spmd, body=%wide.region_0.4_spmd.sunk | while | flops 136840672 | bytes 4672013 | solution.py:54
  46.9 0.6 iota_compare_fusion.4
  47.6 1.4 select_reduce_fusion.2
  51.0 0.6 iota_compare_fusion.4
  51.6 1.4 select_reduce_fusion.2
  55.0 0.6 iota_compare_fusion.4
  55.7 1.4 select_reduce_fusion.2
  59.1 0.6 iota_compare_fusion.4
  59.7 1.4 select_reduce_fusion.2
  64.1 7.1 %all-reduce.3 = s32[32]{0:T(128)S(1)} all-reduce(s32[32]{0:T(128)S(1)} %dynamic-update-slice.3), channel_id=1, replica_groups=mesh['dp'=4,'neg'=8] {'neg'}, use_global_device_ids=true, to_apply=%add.3 | all-reduce | flops 32 | bytes 256
  72.6 11.8 %all-reduce.6 = (f32[256]{0:T(256)S(1)}, f32[256]{0:T(256)S(1)}, f32[256]{0:T(256)S(1)}) all-reduce(f32[256]{0:T(256)S(1)} %dynamic-update-slice.1, f32[256]{0:T(256)S(1)} %dynamic-update-slice.2, f32[256]{0:T(256)S(1)} %dynamic-update-slice.4), channel_id=2, replica_groups=mesh['dp'=4,'neg'=8] {'neg'}, use_global_device_ids=true, to_apply=%add.1 | all-reduce | flops 768 | bytes 6144
  85.0 25.8 %while.55 = (s32[]{:T(128)}, f32[1024,128]{1,0:T(8,128)}, f32[4,512,128]{2,1,0:T(8,128)}, s32[4]{0:T(128)S(1)}, bf16[4,512,128]{2,1,0:T(8,128)(2,1)}, /*index=5*...) while((s32[]{:T(128)}, f32[1024,128]{1,0:T(8,128)}, ...), condition=%wide.region_14.15_spmd.clone, body=%wide.region_13.14_spmd.clone.sunk | while | flops 405012992 | bytes 5282823 | solution.py:114
  85.8 0.6 iota_compare_fusion.5
  86.5 1.5 multiply_convert_fusion.5
  88.0 1.2 fusion.63
  89.1 2.2 convolution_add_fusion.2
  92.1 0.6 iota_compare_fusion.5
  92.8 1.5 multiply_convert_fusion.5
  94.3 1.1 fusion.63
  95.4 2.4 convolution_add_fusion.2
  98.6 0.6 iota_compare_fusion.5
  99.3 1.5 multiply_convert_fusion.5
  100.7 1.1 fusion.63
  101.9 2.4 convolution_add_fusion.2
  105.1 0.6 iota_compare_fusion.5
  105.7 1.5 multiply_convert_fusion.5
  107.2 1.1 fusion.63
  108.4 2.4 convolution_add_fusion.2
  110.8 2.9 fusion.36
  113.8 1.3 copy-done.1
  115.4 21.0 %reduce-scatter.5.cloned.1.call-done = f32[1,512,128]{2,1,0:T(8,128)} async-done(((f32[4,512,128]{2,1,0:T(8,128)}), f32[1,512,128]{2,1,0:T(8,128)}) %reduce-scatter.5.cloned.1.call-update) | async-done | bytes 262160 | tf_op jit(solution)/shard_map/reduce_scatter | solution.py:177
  136.4 2.7 multiply_reduce_fusion
  140.4 3.3 convolution_bitcast_fusion.1
  143.7 1.6 fusion.22
  145.4 85.2 %all-reduce.13.cloned.1.call-done = (f32[1024,1024]{0,1:T(8,128)}, f32[1024,128]{1,0:T(8,128)}) async-done(((f32[1024,1024]{0,1:T(8,128)}, f32[1024,128]{1,0:T(8,128)}), (f32[1024,1024]{0,1:T(8,128)}, f32[1024,128]{1,0:T(8,128)})) %all-reduce.13.cloned.1.call-update) | async-done | bytes 4718608 | tf_op jit(solution)/shard_map/psum | solution.py:10
  231.2 0.7 dynamic-slice_reduce_fusion
  231.8 13.7 %all-reduce.5 = (f32[]{:T(128)}, f32[1024]{0:T(1024)S(1)}) all-reduce(f32[]{:T(128)} %dynamic-slice_reduce_fusion, f32[1024]{0:T(1024)S(1)} %get-tuple-element.355), channel_id=1, replica_groups=mesh['dp'=4,'neg'=8] {'neg'}, use_global_device_ids=true, to_apply=%region_11.12 | all-reduce | flops 1025 | bytes 8200 | tf_op jit(solution)/shard_map/psum | solution.py:10
  245.6 13.7 %all-reduce.8 = (f32[]{:T(128)}, f32[1024]{0:T(1024)}) all-reduce(f32[]{:T(128)} %get-tuple-element.402, f32[1024]{0:T(1024)S(1)} %get-tuple-element.403), channel_id=1, replica_groups=mesh['dp'=4,'neg'=8] {'dp'}, use_global_device_ids=true, to_apply=%region_12.13 | all-reduce | flops 1025 | bytes 8200 | tf_op jit(solution)/shard_map/psum | solution.py:11
  259.9 2.3 convolution_convert_fusion
  262.1 143.4 %all-reduce.15.cloned.1.call-done = (f32[1024,1024]{0,1:T(8,128)}, f32[1024,128]{1,0:T(8,128)}) async-done(((f32[1024,1024]{0,1:T(8,128)}, f32[1024,128]{1,0:T(8,128)}), (f32[1024,1024]{0,1:T(8,128)}, f32[1024,128]{1,0:T(8,128)})) %all-reduce.15.cloned.1.call-update) | async-done | bytes 4718608 | tf_op jit(solution)/shard_map/psum | solution.py:11
  405.5 5.4 %copy.18 = f32[1024,1024]{1,0:T(8,128)} copy(f32[1024,1024]{0,1:T(8,128)} %get-tuple-element.411) | data formatting | bytes 8388608
  410.9 31.2 %reduce-scatter.3.cloned.1.call-done = f32[4,32,128]{2,1,0:T(8,128)} async-done(((f32[32,32,128]{2,1,0:T(8,128)}), f32[4,32,128]{2,1,0:T(8,128)}) %reduce-scatter.3.cloned.1.call-update) | async-done | bytes 65552 | tf_op jit(solution)/shard_map/reduce_scatter | solution.py:176
  442.1 0.8 copy.63
  (123 shorter events, 13.3 us)
Async XLA Ops:
  7.2 103.7 %copy-start = (bf16[1024,1024]{1,0:T(8,128)(2,1)S(1)}, bf16[1024,1024]{1,0:T(8,128)(2,1)}, u32[]{:S(2)}) copy-start(bf16[1024,1024]{1,0:T(8,128)(2,1)} %param.21) | copy-start | bytes 6291460
  7.2 129.3 %reduce-scatter.5.cloned.1.call-start = ((), (), s32[]{:S(2)}) async-start(), calls=%async_computation.3 | async-start | bytes 1310720 | tf_op jit(solution)/shard_map/reduce_scatter | solution.py:177
  46.3 16.2 %copy-start.10 = (u32[32]{0:T(128)S(1)}, u32[32]{0:T(128)}, u32[]{:S(2)}) copy-start(u32[32]{0:T(128)} %constant.164) | copy-start | bytes 388
  46.3 17.5 %copy-start.9 = (s32[4]{0:T(128)S(1)}, s32[4]{0:T(128)}, u32[]{:S(2)}) copy-start(s32[4]{0:T(128)} %param.16) | copy-start | bytes 52
  110.8 119.8 %all-reduce.13.cloned.1.call-start = ((), (), s32[]{:S(2)}) async-start(), calls=%async_computation.4 | async-start | bytes 9437184 | tf_op jit(solution)/shard_map/psum | solution.py:10
  113.7 1.3 copy-start.1
  113.7 22.7 %copy-start.7 = (bf16[1024,128]{1,0:T(8,128)(2,1)S(1)}, bf16[1024,128]{1,0:T(8,128)(2,1)}, u32[]{:S(2)}) copy-start(bf16[1024,128]{1,0:T(8,128)(2,1)} %param.23) | copy-start | bytes 786436
  113.7 22.7 %copy-start.8 = (f32[1024]{0:T(1024)S(1)}, f32[1024]{0:T(1024)}, u32[]{:S(2)}) copy-start(f32[1024]{0:T(1024)} %param.22) | copy-start | bytes 12292
  136.4 2.7 copy-start.2
  139.2 1.2 copy-start.5
  140.4 119.5 %copy-start.3 = (bf16[512,1024]{1,0:T(8,128)(2,1)}, bf16[512,1024]{1,0:T(8,128)(2,1)S(1)}, u32[]{:S(2)}) copy-start(bf16[512,1024]{1,0:T(8,128)(2,1)S(1)} %multiply_convert_fusion.2) | copy-start | bytes 3145732
  140.4 3.3 copy-start.4
  145.3 260.2 %all-reduce.15.cloned.1.call-start = ((), (), s32[]{:S(2)}) async-start(), calls=%async_computation.5 | async-start | bytes 9437184 | tf_op jit(solution)/shard_map/psum | solution.py:11
  230.6 211.5 %reduce-scatter.3.cloned.1.call-start = ((), (), s32[]{:S(2)}) async-start(), calls=%async_computation.2 | async-start | bytes 589824 | tf_op jit(solution)/shard_map/reduce_scatter | solution.py:176
  405.5 36.6 %copy-start.6 = (f32[1024,128]{1,0:T(8,128)S(1)}, f32[1024,128]{1,0:T(8,128)}, u32[]{:S(2)}) copy-start(f32[1024,128]{1,0:T(8,128)} %get-tuple-element.662) | copy-start | bytes 1572868
Sparse Core Ops, SparseCore 0:
  110.9 25.4 reduce-scatter.4
  145.4 85.0 all-reduce.12
  233.0 172.4 all-reduce.14
  409.0 33.0 reduce-scatter.2
